TPU v7x, 8 devices: a whole 2x2x1 slice. The times are simulated.
8 devices in a mesh: part: 1 (over z), row: 2 (over y), col: 4 (over x, core).
Axes of the slice: x: 2, y: 2, z: 1, core: 2. Of those that a mesh axis runs over, the one named last changes fastest.
Arguments:
- ratings: float32 [8192, 512], P(('part', 'row'), 'col')
- mask: int32 [8192, 512], P(('part', 'row'), 'col')
- user_init: float32 [8192, 16], P(('part', 'row'))
- item_init: float32 [512, 16], P(('part', 'col'))
Outputs:
- output 1: float32 [8192, 16], P(('part', 'row'))
- output 2: float32 [512, 16], P(('part', 'col'))
All inputs are finite; a program needn't handle non-finite values.
Results may differ from a plain program's by a relative error of at most 0.00939186.
Values are sent between devices in bfloat16 or wider.
A program may use at most 1 GiB of HBM per device.

v0:
```python
import jax
import jax.numpy as jnp
from jax import lax
from jax.sharding import PartitionSpec as P

CG_STEPS = 4
RIDGE_WEIGHT = 0.0005


def obs_scores(fixed_bf, moving_bf, by_rows):
    if by_rows:
        return lax.dot_general(moving_bf, fixed_bf, (((1,), (1,)), ((), ())), preferred_element_type=jnp.float32)
    return lax.dot_general(fixed_bf, moving_bf, (((1,), (1,)), ((), ())), preferred_element_type=jnp.float32)


def back_product(block_bf, fixed_bf, by_rows):
    contract = 1 if by_rows else 0
    return lax.dot_general(block_bf, fixed_bf, (((contract,), (0,)), ((), ())), preferred_element_type=jnp.float32)


def cg_block(mask_on, ratings_blk, fixed_fac, start, ridge, axis_name, by_rows):
    fixed_bf = fixed_fac.astype(jnp.bfloat16)
    scores = obs_scores(fixed_bf, start.astype(jnp.bfloat16), by_rows)
    resid_obs = jnp.where(mask_on, ratings_blk - scores, 0.0).astype(jnp.bfloat16)
    residual = lax.psum(back_product(resid_obs, fixed_bf, by_rows), axis_name) - ridge * start
    direction = residual
    estimate = start
    res_sq = jnp.sum(residual * residual, axis=1, keepdims=True)
    for cg_step in range(CG_STEPS):
        scores = obs_scores(fixed_bf, direction.astype(jnp.bfloat16), by_rows)
        masked = jnp.where(mask_on, scores.astype(jnp.bfloat16), 0.0)
        gram_dir = lax.psum(back_product(masked, fixed_bf, by_rows), axis_name) + ridge * direction
        step_size = res_sq / jnp.sum(direction * gram_dir, axis=1, keepdims=True)
        estimate = estimate + step_size * direction
        if cg_step + 1 < CG_STEPS:
            residual = residual - step_size * gram_dir
            new_sq = jnp.sum(residual * residual, axis=1, keepdims=True)
            direction = residual + (new_sq / res_sq) * direction
            res_sq = new_sq
    return estimate


def solution(mesh):
    row_size = mesh.shape["row"]
    col_size = mesh.shape["col"]
    grid_spec = P(("part", "row"), "col")
    user_spec = P(("part", "row"), None)
    item_spec = P(("part", "col"), None)

    def local_step(ratings_blk, mask_blk, user_blk, item_blk):
        users_part = ratings_blk.shape[0] * row_size
        items_part = ratings_blk.shape[1] * col_size
        mask_on = mask_blk > 0
        user_new = cg_block(mask_on, ratings_blk, item_blk, user_blk, RIDGE_WEIGHT * items_part, "col", True)
        item_new = cg_block(mask_on, ratings_blk, user_new, item_blk, RIDGE_WEIGHT * users_part, "row", False)
        return user_new, item_new

    return jax.shard_map(local_step, mesh=mesh, in_specs=(grid_spec, grid_spec, user_spec, item_spec), out_specs=(user_spec, item_spec), check_vma=False)
```

profile of v0, /device:TPU:0, one launch (start us, length us, event | category | flops | bytes accessed | tf_op | source)
XLA Modules:
  0.0 206.9 jit_solution(4304569692546990199)
XLA Ops:
  8.1 1.9 broadcast_compare_fusion
  10.0 1.6 fusion.21
  11.6 29.5 %all-reduce.6.cloned.1.call-done = f32[4096,16]{0,1:T(8,128)} async-done(((f32[4096,16]{0,1:T(8,128)}), f32[4096,16]{0,1:T(8,128)}) %all-reduce.6.cloned.1.call-update) | async-done | bytes 262160 | tf_op jit(solution)/shard_map/psum | solution.py:25
  42.1 1.6 fusion.19
  43.8 26.9 %all-reduce.8.cloned.1.call-done = f32[4096,16]{0,1:T(8,128)} async-done(((f32[4096,16]{0,1:T(8,128)}), f32[4096,16]{0,1:T(8,128)}) %all-reduce.8.cloned.1.call-update) | async-done | bytes 262160 | tf_op jit(solution)/shard_map/psum | solution.py:32
  70.7 1.1 multiply_reduce_fusion.6
  72.9 2.5 %fusion.18 = f32[4096,16]{0,1:T(8,128)} fusion(bf16[128,16]{0,1:T(8,128)(2,1)S(1)} %convert_element_type.74, pred[4096,128]{1,0:T(32,128)(4,1)S(1)} %broadcast_compare_fusion, f32[4096,16]{0,1:T(8,128)S(1)} %multiply_subtract_fusion.3, f32[4096]{0:T(1024)S(1)} %div.113, f32[4096,16]{0,1:T(8,128)} %all-reduce.8.cloned.1.call-done, f32[4096]{0:T(1024)S(1)} %div.112), kind=kOutput, calls=%fused_computation.28 | convolution fusion | flops 35061760 | bytes 1347584 | tf_op jit(solution)/shard_map/dot_general | solution.py:18
  75.5 26.7 %all-reduce.10.cloned.1.call-done = f32[4096,16]{0,1:T(8,128)} async-done(((f32[4096,16]{0,1:T(8,128)}), f32[4096,16]{0,1:T(8,128)}) %all-reduce.10.cloned.1.call-update) | async-done | bytes 262160 | tf_op jit(solution)/shard_map/psum | solution.py:32
  102.2 1.1 multiply_reduce_fusion.4
  103.3 1.1 multiply_reduce_fusion.3
  105.2 1.6 fusion.17
  106.8 26.7 %all-reduce.12.cloned.1.call-done = f32[4096,16]{0,1:T(8,128)} async-done(((f32[4096,16]{0,1:T(8,128)}), f32[4096,16]{0,1:T(8,128)}) %all-reduce.12.cloned.1.call-update) | async-done | bytes 262160 | tf_op jit(solution)/shard_map/psum | solution.py:32
  134.6 1.1 multiply_reduce_fusion.1
  135.7 1.8 multiply_add_fusion.1
  137.5 2.5 %fusion.16 = f32[4096,16]{0,1:T(8,128)} fusion(bf16[128,16]{0,1:T(8,128)(2,1)S(1)} %convert_element_type.74, pred[4096,128]{1,0:T(32,128)(4,1)S(1)} %broadcast_compare_fusion, f32[4096,16]{0,1:T(8,128)} %multiply_add_fusion.1), kind=kOutput, calls=%fused_computation.26 | convolution fusion | flops 34668544 | bytes 1052672 | tf_op jit(solution)/shard_map/dot_general | solution.py:18
  140.0 26.8 %all-reduce.14.cloned.1.call-done = f32[4096,16]{0,1:T(8,128)} async-done(((f32[4096,16]{0,1:T(8,128)}), f32[4096,16]{0,1:T(8,128)}) %all-reduce.14.cloned.1.call-update) | async-done | bytes 262160 | tf_op jit(solution)/shard_map/psum | solution.py:32
  166.8 1.1 multiply_reduce_fusion
  167.9 1.9 fusion.60
  169.8 1.5 fusion.20
  171.3 5.0 %psum.75 = f32[128,16]{0,1:T(8,128)S(1)} all-reduce(f32[128,16]{0,1:T(8,128)S(1)} %fusion.20), channel_id=1, replica_groups=mesh['part'=1,'row'=2,'col'=4] {'row'}, use_global_device_ids=true, to_apply=%region_13.14 | all-reduce | flops 2048 | bytes 16384 | tf_op jit(solution)/shard_map/psum | solution.py:25
  177.1 5.0 %psum.76 = f32[128,16]{0,1:T(8,128)S(1)} all-reduce(f32[128,16]{0,1:T(8,128)S(1)} %fusion.15), channel_id=1, replica_groups=mesh['part'=1,'row'=2,'col'=4] {'row'}, use_global_device_ids=true, to_apply=%region_15.16 | all-reduce | flops 2048 | bytes 16384 | tf_op jit(solution)/shard_map/psum | solution.py:32
  183.0 5.1 %psum.77 = f32[128,16]{0,1:T(8,128)S(1)} all-reduce(f32[128,16]{0,1:T(8,128)S(1)} %fusion.14), channel_id=1, replica_groups=mesh['part'=1,'row'=2,'col'=4] {'row'}, use_global_device_ids=true, to_apply=%region_18.19 | all-reduce | flops 2048 | bytes 16384 | tf_op jit(solution)/shard_map/psum | solution.py:32
  188.9 5.0 %psum.78 = f32[128,16]{0,1:T(8,128)S(1)} all-reduce(f32[128,16]{0,1:T(8,128)S(1)} %fusion.13), channel_id=1, replica_groups=mesh['part'=1,'row'=2,'col'=4] {'row'}, use_global_device_ids=true, to_apply=%region_21.22 | all-reduce | flops 2048 | bytes 16384 | tf_op jit(solution)/shard_map/psum | solution.py:32
  194.8 5.0 %psum.79 = f32[128,16]{0,1:T(8,128)S(1)} all-reduce(f32[128,16]{0,1:T(8,128)S(1)} %fusion.12), channel_id=1, replica_groups=mesh['part'=1,'row'=2,'col'=4] {'row'}, use_global_device_ids=true, to_apply=%region_24.25 | all-reduce | flops 2048 | bytes 16384 | tf_op jit(solution)/shard_map/psum | solution.py:32
  (62 shorter events, 9.0 us)
Async XLA Ops:
  7.2 2.8 %copy-start.3 = (f32[4096,16]{0,1:T(8,128)S(1)}, f32[4096,16]{0,1:T(8,128)}, u32[]{:S(2)}) copy-start(f32[4096,16]{0,1:T(8,128)} %param.6) | copy-start | bytes 786436
  7.2 2.8 %copy-start.1 = (f32[4096,128]{1,0:T(8,128)S(1)}, f32[4096,128]{1,0:T(8,128)}, u32[]{:S(2)}) copy-start(f32[4096,128]{1,0:T(8,128)} %param.4) | copy-start | bytes 6291460
  7.2 34.0 %all-reduce.6.cloned.1.call-start = ((), (), s32[]{:S(2)}) async-start(), calls=%async_computation | async-start | bytes 524288 | tf_op jit(solution)/shard_map/psum | solution.py:25
  8.1 129.4 %copy-start.8 = (bf16[128,16]{0,1:T(8,128)(2,1)}, bf16[128,16]{0,1:T(8,128)(2,1)S(1)}, u32[]{:S(2)}) copy-start(bf16[128,16]{0,1:T(8,128)(2,1)S(1)} %convert_element_type.74) | copy-start | bytes 12292
  11.6 59.1 %all-reduce.8.cloned.1.call-start = ((), (), s32[]{:S(2)}) async-start(), calls=%async_computation.1 | async-start | bytes 524288 | tf_op jit(solution)/shard_map/psum | solution.py:32
  43.7 58.5 %all-reduce.10.cloned.1.call-start = ((), (), s32[]{:S(2)}) async-start(), calls=%async_computation.2 | async-start | bytes 524288 | tf_op jit(solution)/shard_map/psum | solution.py:32
  70.7 31.5 %copy-start = (f32[4096,16]{0,1:T(8,128)S(1)}, f32[4096,16]{0,1:T(8,128)}, u32[]{:S(2)}) copy-start(f32[4096,16]{0,1:T(8,128)} %all-reduce.8.cloned.1.call-done) | copy-start | bytes 786436
  72.9 32.3 %copy-start.4 = (f32[4096]{0:T(1024)}, f32[4096]{0:T(1024)S(1)}, u32[]{:S(2)}) copy-start(f32[4096]{0:T(1024)S(1)} %div.113) | copy-start | bytes 49156
  75.4 58.1 %all-reduce.12.cloned.1.call-start = ((), (), s32[]{:S(2)}) async-start(), calls=%async_computation.3 | async-start | bytes 524288 | tf_op jit(solution)/shard_map/psum | solution.py:32
  103.3 31.3 %copy-start.6 = (f32[4096]{0:T(1024)}, f32[4096]{0:T(1024)S(1)}, u32[]{:S(2)}) copy-start(f32[4096]{0:T(1024)S(1)} %div.114) | copy-start | bytes 49156
  104.4 0.7 copy-start.2
  106.8 60.0 %all-reduce.14.cloned.1.call-start = ((), (), s32[]{:S(2)}) async-start(), calls=%async_computation.4 | async-start | bytes 524288 | tf_op jit(solution)/shard_map/psum | solution.py:32
  134.6 33.3 %copy-start.5 = (f32[4096]{0:T(1024)}, f32[4096]{0:T(1024)S(1)}, u32[]{:S(2)}) copy-start(f32[4096]{0:T(1024)S(1)} %div.116) | copy-start | bytes 49156
  169.8 6.5 %copy-start.7 = (f32[128,16]{0,1:T(8,128)S(1)}, f32[128,16]{0,1:T(8,128)}, u32[]{:S(2)}) copy-start(f32[128,16]{0,1:T(8,128)} %param.7) | copy-start | bytes 24580
Sparse Core Ops, SparseCore 0:
  11.7 29.4 all-reduce.5
  44.0 26.5 all-reduce.7
  75.5 26.5 all-reduce.9
  106.9 26.5 all-reduce.11
  140.2 26.5 all-reduce.13
where the time goes:
time: 208 us; the launch traced here: 207 us
  waiting for transfers between devices  137 us (66%)
  blocking collectives  25.1 us (12%)
  other arithmetic  16 us (8%)
  matrix products  14.3 us (7%)
  between operations  14 us (7%)
    psum x4, waiting for transfers between devices, cg_block(): lax.psum(back_product(masked, fixed_bf, by_rows), axis_name)  107 us
    psum x1, waiting for transfers between devices, cg_block(): lax.psum(back_product(resid_obs, fixed_bf, by_rows), axis_name)  29.5 us
    psum x4, blocking collectives, cg_block(): lax.psum(back_product(masked, fixed_bf, by_rows), axis_name)  20.1 us
    dot_general x10, matrix products, back_product(): lax.dot_general(block_bf, fixed_bf, (((contract,), (0,)), ((), ())), pref...  14.3 us
    psum x1, blocking collectives, cg_block(): lax.psum(back_product(resid_obs, fixed_bf, by_rows), axis_name)  4.99 us
    reduce_sum x8, other arithmetic, cg_block(): step_size = res_sq / jnp.sum(direction * gram_dir, axis=1, keepdims=True)  4.4 us
  transfers between devices with their start and end apart: 5, of which 5 were waited for; matrix products, arithmetic and copies ran while one was open for 0% of the time, Pallas kernels for 0%

commit v1 on v0

v1 whole, which is shorter than its diff:
```python
import functools

import jax
import jax.numpy as jnp
from jax import lax
from jax.experimental import pallas as pl
from jax.experimental.pallas import tpu as pltpu
from jax.sharding import PartitionSpec as P

CG_STEPS = 4
RIDGE_WEIGHT = 0.0005
RANK = 16
DIAGS = RANK // 2 + 1
MESH = pl.DeviceIdType.MESH
F32 = jnp.float32
BF16 = jnp.bfloat16
COLS = 4
CHUNKS = 4


def dot_nt(a, b):
    return lax.dot_general(a, b, (((1,), (1,)), ((), ())), preferred_element_type=F32)


def dot_nn(a, b):
    return lax.dot_general(a, b, (((1,), (0,)), ((), ())), preferred_element_type=F32)


def turn(x, shift):
    return x if shift % RANK == 0 else pltpu.roll(x, shift % RANK, 0)


def pair_products(fac):
    prods = jnp.concatenate([fac * turn(fac, -d) for d in range(DIAGS)], axis=0)
    high = prods.astype(BF16)
    low = (prods - high.astype(F32)).astype(BF16)
    return high, low


def apply_gram(diags, vec):
    out = diags[0] * vec
    for d in range(1, DIAGS):
        out = out + diags[d] * turn(vec, -d)
        if d < RANK // 2:
            out = out + turn(diags[d] * vec, d)
    return out


def cg_solve(diags, residual, start, ridge):
    direction = residual
    estimate = start
    res_sq = jnp.sum(residual * residual, axis=0, keepdims=True)
    for cg_step in range(CG_STEPS):
        gram_dir = apply_gram(diags, direction) + ridge * direction
        step_size = res_sq / jnp.sum(direction * gram_dir, axis=0, keepdims=True)
        estimate = estimate + step_size * direction
        if cg_step + 1 < CG_STEPS:
            residual = residual - step_size * gram_dir
            new_sq = jnp.sum(residual * residual, axis=0, keepdims=True)
            direction = residual + (new_sq / res_sq) * direction
            res_sq = new_sq
    return estimate


def sweep_kernel(
    user_ridge, item_ridge,
    ratings_hbm, mask_hbm, user_hbm, item_hbm,
    user_out, item_out,
    rate, mask32, user0, item0,
    mask16, mask16_peer, item16, item16_peer, ffs,
    gram_send, gram_recv, gram_own,
    res_pair, res_pair_recv, res_far, res_far_recv, res_own,
    fac, user1, item_send, item_recv,
    in_sem, out_sem, item_sem, mask_sem, pair_sem, far_sem, gram_sem, fac_sem, user_sem, cross_sem,
):
    part = lax.axis_index("part")
    row = lax.axis_index("row")
    col = lax.axis_index("col")
    chip = col // 2
    core = col % 2
    pair_col = chip * 2 + (1 - core)
    far_col = (1 - chip) * 2 + core
    diag_col = (1 - chip) * 2 + (1 - core)
    pair = (part, row, pair_col)
    far = (part, row, far_col)
    diag = (part, row, diag_col)
    cross = (part, 1 - row, col)

    span = mask16.shape[1]
    width = span // CHUNKS
    items = item0.shape[1]

    def copy_to(src, dst, sems, slot, device):
        return pltpu.make_async_remote_copy(
            src_ref=src, dst_ref=dst, send_sem=sems.at[0, slot], recv_sem=sems.at[1, slot],
            device_id=device, device_id_type=MESH,
        )

    barrier = pltpu.get_barrier_semaphore()
    for device in (pair, far, diag, cross):
        pl.semaphore_signal(barrier, inc=1, device_id=device, device_id_type=MESH)

    order = (diag_col, far_col, pair_col, col)

    def load(src, dst, slot):
        return pltpu.make_async_copy(src, dst, in_sem.at[slot])

    loads = [load(item_hbm, item0, 0)]
    for slot, block in enumerate(order):
        rows = pl.ds(pl.multiple_of(block * span, span), span)
        loads.append(load(mask_hbm.at[rows], mask32.at[slot], 1 + slot))
    loads.append(load(user_hbm, user0, 5))
    for slot, block in enumerate(order):
        rows = pl.ds(pl.multiple_of(block * span, span), span)
        loads.append(load(ratings_hbm.at[rows], rate.at[slot], 6 + slot))
    for copy in loads:
        copy.start()

    loads[0].wait()
    item16[...] = item0[...].astype(BF16)
    high, low = pair_products(item16[...].astype(F32))
    ffs[0, :, :items] = high
    ffs[0, :, items:] = low
    loads[1].wait()
    mask16[0] = mask32[0].astype(F32).astype(BF16)
    pl.semaphore_wait(barrier, 4)
    item_copy = copy_to(item16, item16_peer, item_sem, 0, pair)
    item_copy.start()
    mask_copies = [copy_to(mask16.at[0], mask16_peer.at[0], mask_sem, 0, pair)]
    mask_copies[0].start()
    loads[2].wait()
    mask16[1] = mask32[1].astype(F32).astype(BF16)
    loads[3].wait()
    mask16[2] = mask32[2].astype(F32).astype(BF16)
    mask_copies.append(copy_to(mask16.at[2], mask16_peer.at[1], mask_sem, 1, pair))
    mask_copies[1].start()
    loads[4].wait()
    mask16[3] = mask32[3].astype(F32).astype(BF16)

    item_copy.wait_recv()
    high, low = pair_products(item16_peer[...].astype(F32))
    ffs[1, :, :items] = high
    ffs[1, :, items:] = low

    def gram_part(slot, chunk):
        mine = mask16[slot, pl.ds(chunk * width, width), :]
        peer = mask16_peer[slot // 2, pl.ds(chunk * width, width), :]
        total = dot_nt(ffs[0], jnp.concatenate([mine, mine], axis=1))
        return total + dot_nt(ffs[1], jnp.concatenate([peer, peer], axis=1))

    mask_copies[0].wait_recv()
    gram_copies = []
    for chunk in range(CHUNKS):
        gram_send[chunk] = gram_part(1, chunk).astype(BF16)
        gram_copies.append(copy_to(gram_send.at[chunk], gram_recv.at[chunk], gram_sem, chunk, far))
        gram_copies[-1].start()

    loads[5].wait()

    def user_residual(slot, block):
        start = user0[:, pl.ds(pl.multiple_of(block * span, span), span)]
        scores = dot_nn(start.T.astype(BF16), item16[...])
        resid = jnp.where(mask32[slot] > 0, rate[slot] - scores, 0.0).astype(BF16)
        return dot_nt(item16[...], resid)

    loads[6].wait()
    res_pair[0] = user_residual(0, diag_col)
    pair_copies = [copy_to(res_pair.at[0], res_pair_recv.at[0], pair_sem, 0, pair)]
    pair_copies[0].start()
    loads[8].wait()
    res_pair[1] = user_residual(2, pair_col)
    pair_copies.append(copy_to(res_pair.at[1], res_pair_recv.at[1], pair_sem, 1, pair))
    pair_copies[1].start()
    loads[7].wait()
    far_part = user_residual(1, far_col)
    pair_copies[0].wait_recv()
    res_far[...] = far_part + res_pair_recv[0]
    far_copy = copy_to(res_far, res_far_recv, far_sem, 0, far)
    far_copy.start()
    loads[9].wait()
    own_part = user_residual(3, col)
    mask_copies[1].wait_recv()
    for chunk in range(CHUNKS):
        gram_own[chunk] = gram_part(3, chunk)
    pair_copies[1].wait_recv()
    mine0 = user0[:, pl.ds(pl.multiple_of(col * span, span), span)]
    res_own[...] = own_part + res_pair_recv[1] - user_ridge * mine0

    def item_part(source, slot, chunk, acc):
        factors = fac[source, chunk]
        wide = factors.astype(F32)
        rows = pl.ds(chunk * width, width)
        seen = mask16[slot, rows, :]
        high, low = pair_products(wide)
        gram = dot_nn(high, seen) + dot_nn(low, seen)
        scores = dot_nn(wide.T.astype(BF16), item16[...])
        resid = jnp.where(mask32[slot, rows, :] > 0, rate[slot, rows, :] - scores, 0.0).astype(BF16)
        part_sum = jnp.concatenate([gram, dot_nn(factors, resid)], axis=0)
        return part_sum if acc is None else acc + part_sum

    far_copy.wait_recv()
    sums = None
    fac_copies = []
    user_copies = []
    peers = ((0, pair, pair_col, 2), (1, far, far_col, 1), (2, diag, diag_col, 0))

    def gather(chunk, acc):
        for lane, _, source, slot in peers:
            fac_copies[chunk][lane].wait_recv()
            acc = item_part(source, slot, chunk, acc)
        return acc

    for chunk in range(CHUNKS):
        lanes = pl.ds(chunk * width, width)
        gram_copies[chunk].wait_recv()
        full = gram_own[chunk] + gram_recv[chunk].astype(F32)
        diags = [full[d * RANK:(d + 1) * RANK] for d in range(DIAGS)]
        start = user0[:, pl.ds(pl.multiple_of(col * span + chunk * width, width), width)]
        solved = cg_solve(diags, res_own[:, lanes] + res_far_recv[:, lanes], start, user_ridge)
        fac[col, chunk] = solved.astype(BF16)
        user1[col, chunk] = solved
        sent = []
        for lane, device, _, _ in peers:
            sent.append(copy_to(fac.at[col, chunk], fac.at[col, chunk], fac_sem, chunk * 3 + lane, device))
            sent[-1].start()
        fac_copies.append(sent)
        whole = []
        for lane, device, _, _ in peers:
            whole.append(copy_to(user1.at[col, chunk], user1.at[col, chunk], user_sem, chunk * 3 + lane, device))
            whole[-1].start()
        user_copies.append(whole)
        sums = item_part(col, 3, chunk, sums)
        if chunk:
            sums = gather(chunk - 1, sums)
    sums = gather(CHUNKS - 1, sums)
    item_send[...] = sums
    cross_copy = copy_to(item_send, item_recv, cross_sem, 0, cross)
    cross_copy.start()

    outs = []
    for chunk in range(CHUNKS):
        for lane in range(3):
            user_copies[chunk][lane].wait_recv()
        for source in range(COLS):
            dst = user_out.at[:, pl.ds(source * span + chunk * width, width)]
            outs.append(pltpu.make_async_copy(user1.at[source, chunk], dst, out_sem.at[chunk * COLS + source]))
            outs[-1].start()

    cross_copy.wait_recv()
    full = item_send[...] + item_recv[...]
    diags = [full[d * RANK:(d + 1) * RANK] for d in range(DIAGS)]
    residual = full[DIAGS * RANK:] - item_ridge * item0[...]
    item_out[...] = cg_solve(diags, residual, item0[...], item_ridge)

    for copy in outs:
        copy.wait()
    for copy in [item_copy, far_copy, cross_copy] + mask_copies + pair_copies + gram_copies + sum(fac_copies, []) + sum(user_copies, []):
        copy.wait_send()


def solution(mesh):
    row_size = mesh.shape["row"]
    col_size = mesh.shape["col"]
    grid_spec = P(("part", "row"), "col")
    user_spec = P(("part", "row"), None)
    item_spec = P(("part", "col"), None)

    def local_step(ratings_blk, mask_blk, user_blk, item_blk):
        users, items = ratings_blk.shape
        span = users // COLS
        width = span // CHUNKS
        any_spec = pl.BlockSpec(memory_space=pl.ANY)
        vmem = pltpu.VMEM
        dma = pltpu.SemaphoreType.DMA
        terms = DIAGS * RANK
        user_new, item_new = pl.pallas_call(
            functools.partial(sweep_kernel, RIDGE_WEIGHT * items * col_size, RIDGE_WEIGHT * users * row_size),
            out_shape=(
                jax.ShapeDtypeStruct((RANK, users), F32),
                jax.ShapeDtypeStruct((RANK, items), F32),
            ),
            in_specs=[any_spec] * 4,
            out_specs=(any_spec, pl.BlockSpec(memory_space=pltpu.VMEM)),
            scratch_shapes=[
                vmem((COLS, span, items), F32),
                vmem((COLS, span, items), jnp.int32),
                vmem((RANK, users), F32),
                vmem((RANK, items), F32),
                vmem((COLS, span, items), BF16),
                vmem((2, span, items), BF16),
                vmem((RANK, items), BF16),
                vmem((RANK, items), BF16),
                vmem((2, terms, 2 * items), BF16),
                vmem((CHUNKS, terms, width), BF16),
                vmem((CHUNKS, terms, width), BF16),
                vmem((CHUNKS, terms, width), F32),
                vmem((2, RANK, span), F32),
                vmem((2, RANK, span), F32),
                vmem((RANK, span), F32),
                vmem((RANK, span), F32),
                vmem((RANK, span), F32),
                vmem((COLS, CHUNKS, RANK, width), BF16),
                vmem((COLS, CHUNKS, RANK, width), F32),
                vmem((terms + RANK, items), F32),
                vmem((terms + RANK, items), F32),
                dma((10,)),
                dma((COLS * CHUNKS,)),
                dma((2, 1)),
                dma((2, 2)),
                dma((2, 2)),
                dma((2, 1)),
                dma((2, CHUNKS)),
                dma((2, CHUNKS * 3)),
                dma((2, CHUNKS * 3)),
                dma((2, 1)),
            ],
            compiler_params=pltpu.CompilerParams(collective_id=0, has_side_effects=True),
        )(ratings_blk, mask_blk, user_blk.T, item_blk.T)
        return user_new.T, item_new.T

    return jax.shard_map(local_step, mesh=mesh, in_specs=(grid_spec, grid_spec, user_spec, item_spec), out_specs=(user_spec, item_spec), check_vma=False)
```

time: 208 us -> 33.3 us (0.16)
  waiting for transfers between devices: 137 us -> 0 us
  Pallas kernels: 0 us -> 29.5 us
  blocking collectives: 25.1 us -> 0 us
  other arithmetic: 16 us -> 0 us
  matrix products: 14.3 us -> 0 us
  between operations: 14 us -> 0.64 us
  local copies, waits for them, and re-layouts: 0.72 us -> 2.97 us
    psum x5 -> x0, waiting for transfers between devices: 137 us -> none  [the longest x4 107 us: cg_block(): lax.psum(back_product(masked, fixed_bf, by_rows), axis_name)]
    pallas_call x0 -> x1, Pallas kernels: none -> 29.5 us  [local_step(): pl.pallas_call(functools.partial(sweep_kernel, RIDGE_WEIGHT * items * col...]
    psum x5 -> x0, blocking collectives: 25.1 us -> none  [the longest x4 20.1 us: cg_block(): lax.psum(back_product(masked, fixed_bf, by_rows), axis_name)]
    dot_general x10 -> x0, matrix products: 14.3 us -> none  [back_product(): lax.dot_general(block_bf, fixed_bf, (((contract,), (0,)), ((), ())), pref...]
    reduce_sum x14 -> x0, other arithmetic: 7.71 us -> none  [the longest x8 4.4 us: cg_block(): step_size = res_sq / jnp.sum(direction * gram_dir, axis=1, keepdims=True)]
    convert_element_type x2 -> x0, other arithmetic: 2.77 us -> none  [cg_block(): fixed_bf = fixed_fac.astype(jnp.bfloat16)]
    add x5 -> x0, other arithmetic: 2.51 us -> none  [the longest x4 1.9 us: cg_block(): direction = residual + new_sq / res_sq * direction]
    unnamed x18 -> x2, local copies, waits for them, and re-layouts: 0.72 us -> 2.97 us
  transfers between devices with their start and end apart: 5 -> 0, of which waited for: 5 -> 0; matrix products, arithmetic and copies ran while one was open for 0% -> 0% of each run, Pallas kernels for 0% -> 0%
where the time goes in v1:
time: 33.3 us; the launch traced here: 33.1 us
  Pallas kernels  29.5 us (89%)
  local copies, waits for them, and re-layouts  2.97 us (9%)
  between operations  0.64 us (2%)
    pallas_call x1, Pallas kernels, local_step(): pl.pallas_call(functools.partial(sweep_kernel, RIDGE_WEIGHT * items * col...  29.5 us
    unnamed x2, local copies, waits for them, and re-layouts  2.97 us

profile of v1, /device:TPU:0, one launch (start us, length us, event | category | flops | bytes accessed | tf_op | source)
XLA Modules:
  0.0 33.1 jit_solution(13629312584815334993)
XLA Ops:
  0.6 29.5 %shard_map.59 = (f32[16,4096]{1,0:T(8,128)}, f32[16,128]{1,0:T(8,128)}) custom-call(f32[4096,128]{1,0:T(8,128)} %ratings_hbm.1, s32[4096,128]{1,0:T(8,128)} %mask_hbm.1, f32[16,4096]{1,0:T(8,128)} %bitcast.4, f32[16,128]{1,0:T(8,128)} %bitcast.6), custom_call_target="tpu_custom_call" | custom-call | tf_op jit(solution)/shard_map/pallas_call | solution.py:276
  30.2 1.7 %copy.8 = f32[4096,16]{0,1:T(8,128)} copy(f32[4096,16]{0,1:T(8,128)} %bitcast.5) | data formatting | bytes 524288
  31.8 1.3 %copy.9 = f32[128,16]{0,1:T(8,128)} copy(f32[128,16]{0,1:T(8,128)} %bitcast.7) | data formatting | bytes 16384
